TPU v7x, 32 devices: a whole 2x2x4 slice. The times are simulated.
32 devices in a mesh: re: 4 (over y, x), ka: 8 (over z, core).
Axes of the slice: x: 2, y: 2, z: 4, core: 2. Of those that a mesh axis runs over, the one named last changes fastest.
Arguments:
- lattice_blocks: bfloat16 [192, 2, 3, 256], P(('re', 'ka')), may hold values from -0.4375 to 0.4375
- lattice_coords: int32 [192, 3], P(('re', 'ka')), may hold values from -8 to 8
- kpoint_index: int32 [192, 3], P('ka'), may hold values from 0 to 63
- polarization: float32 [3], replicated, may hold values from -4 to 4
- energy_gap: float32 [192, 32], P('ka'), may hold values from 0.5 to 2.5
- coupling: bfloat16 [8, 96, 2, 32, 8], P('ka', 're'), may hold values from -1 to 1
- phonon_weight: bfloat16 [8, 96], P('ka', 're'), may hold values from 0.19921875 to 5
Outputs:
- rates: float32 [192, 8], P('ka', 're')
All inputs are finite; a program needn't handle non-finite values.
Results may differ from a plain program's by a relative error of at most 0.0014.
Values may be sent and summed in bfloat16 or wider, within the bound.
A program may use at most 128 MiB of HBM per device.

v0:
```python
import math
import jax
import jax.numpy as jnp
from jax import lax
from jax.sharding import PartitionSpec as P

NV = 8
NC = 8
NMODE = 96
NKG = 64


def phase_rows(kpoint_index, coords):
    turns = jnp.mod(jnp.sum(kpoint_index[:, None, :] * coords[None, :, :], axis=2), NKG)
    angle = turns.astype(jnp.float32) * (2.0 * math.pi / NKG)
    cosine = jnp.cos(angle).astype(jnp.bfloat16)
    sine = jnp.sin(angle).astype(jnp.bfloat16)
    count = kpoint_index.shape[0]
    upper = jnp.stack([cosine, -sine], axis=2).reshape(count, -1)
    lower = jnp.stack([sine, cosine], axis=2).reshape(count, -1)
    return jnp.concatenate([upper, lower], axis=0)


def left_factor(momenta, polarization, energy_gap):
    count = momenta.shape[1]
    parts = momenta.reshape(2, count, 3, NV, -1)
    along = (
        parts[:, :, 0] * polarization[0]
        + parts[:, :, 1] * polarization[1]
        + parts[:, :, 2] * polarization[2]
    )
    return (along / energy_gap[None, :, None, :]).astype(jnp.bfloat16).reshape(2, count * NV, -1)


def rate_block(factor, coup, weight):

    def product(left, right):
        return jnp.einsum("qvmj,am->qvja", right, left, preferred_element_type=jnp.float32)

    real_left, imag_left = (factor[0], factor[1])
    real_right, imag_right = (coup[:, :, 0], coup[:, :, 1])
    are = product(real_left, real_right) - product(imag_left, imag_right)
    aim = product(real_left, imag_right) + product(imag_left, real_right)
    power = (are * are + aim * aim) * weight.astype(jnp.float32)[:, :, None, None]
    summed = jnp.sum(power, axis=(1, 2))
    count = factor.shape[1] // NV
    qcount = coup.shape[0]
    return jnp.sum(summed.reshape(qcount, count, NV), axis=2).T * (1.0 / (NMODE * NV * NC))


def body(
    lattice_blocks, lattice_coords, kpoint_index, polarization, energy_gap, coupling, phonon_weight
):
    own_count = kpoint_index.shape[0]
    cols = lattice_blocks.shape[2] * lattice_blocks.shape[3]
    blocks = lax.all_gather(lattice_blocks, "ka", axis=0, tiled=True)
    coords = lax.all_gather(lattice_coords.astype(jnp.bfloat16), "ka", axis=0, tiled=True)
    left = phase_rows(kpoint_index, coords.astype(jnp.int32))
    partial_value = jnp.dot(left, blocks.reshape(-1, cols), preferred_element_type=jnp.float32)
    momenta = lax.psum(partial_value, "re").reshape(2, own_count, cols)
    factor = left_factor(momenta, polarization, energy_gap)
    partial_rates = rate_block(
        factor,
        lax.all_gather(coupling, "ka", axis=0, tiled=True),
        lax.all_gather(phonon_weight, "ka", axis=0, tiled=True),
    )
    return lax.psum_scatter(partial_rates, "re", scatter_dimension=1, tiled=True)


def solution(mesh):
    return jax.shard_map(
        body,
        mesh=mesh,
        in_specs=(
            P(("re", "ka"), None, None, None),
            P(("re", "ka"), None),
            P("ka", None),
            P(),
            P("ka", None),
            P("ka", "re", None, None, None),
            P("ka", "re"),
        ),
        out_specs=P("ka", "re"),
        check_vma=False,
    )
```

profile of v0, /device:TPU:0, one launch (start us, length us, event | category | flops | bytes accessed | tf_op | source)
XLA Modules:
  0.0 103.5 jit_solution(17837021338715821611)
XLA Ops:
  6.5 0.0 all-reduce.3.cloned.1.call-start
  6.5 0.7 convert_bitcast_fusion
  7.2 13.5 %all-gather = bf16[8,6,3]{1,2,0:T(4,128)(2,1)S(1)} all-gather(bf16[1,6,3]{1,2,0:T(4,128)(2,1)S(1)} %convert_bitcast_fusion), channel_id=1, replica_groups=mesh['re'=4,'ka'=8] {'ka'}, dimensions={0}, use_global_device_ids=true | all-gather | bytes 324 | tf_op jit(solution)/shard_map/all_gather | solution.py:57
  20.7 0.1 reshape.103
  20.8 0.8 multiply_reduce_fusion.1
  21.5 0.1 fusion.16
  21.6 0.1 cosine_convert_fusion
  21.7 0.1 copy.53
  21.8 0.1 copy.54
  21.9 14.2 %all_gather.13 = bf16[48,2,3,256]{3,1,2,0:T(2,128)(2,1)S(1)} all-gather(bf16[6,2,3,256]{3,1,2,0:T(2,128)(2,1)} %param.7), channel_id=1, replica_groups=mesh['re'=4,'ka'=8] {'ka'}, dimensions={0}, use_global_device_ids=true | all-gather | bytes 165888 | tf_op jit(solution)/shard_map/all_gather | solution.py:56
  36.1 0.1 copy.55
  36.2 0.0 copy-start
  36.2 0.3 fusion.8
  36.5 0.2 reshape_reshape.3
  36.7 0.0 copy-start.3
  36.7 0.0 copy-start.4
  36.7 0.0 copy-start.2
  36.8 0.0 copy-start.1
  36.8 0.8 copy.56
  37.6 0.0 all-reduce.3.cloned.1.call-update
  37.6 0.0 copy-done
  37.7 16.3 %all_gather.14 = bf16[8,24,2,32,8]{3,1,4,0,2:T(8,128)(2,1)S(1)} all-gather(bf16[1,24,2,32,8]{3,1,4,0,2:T(8,128)(2,1)S(1)} %copy.57), channel_id=1, replica_groups=mesh['re'=4,'ka'=8] {'ka'}, dimensions={0}, use_global_device_ids=true | all-gather | bytes 221184 | tf_op jit(solution)/shard_map/all_gather | solution.py:64
  53.9 0.0 copy-done.3
  53.9 8.7 %all-gather.1 = bf16[8,1,24]{2,1,0:T(2,128)(2,1)S(1)} all-gather(bf16[1,1,24]{2,1,0:T(2,128)(2,1)S(1)} %bitcast.62), channel_id=1, replica_groups=mesh['re'=4,'ka'=8] {'ka'}, dimensions={0}, use_global_device_ids=true | all-gather | bytes 432 | tf_op jit(solution)/shard_map/all_gather | solution.py:65
  62.7 0.0 copy-done.4
  62.7 0.6 dynamic-slice
  63.9 0.0 copy-done.2
  63.9 0.6 fusion.17
  64.6 17.4 %all-reduce.3.cloned.1.call-done = f32[2,24,3,8,32]{4,3,1,0,2:T(8,128)} async-done(((f32[2,24,3,8,32]{4,3,1,0,2:T(8,128)}), f32[2,24,3,8,32]{4,3,1,0,2:T(8,128)}) %all-reduce.3.cloned.1.call-update) | async-done | bytes 147472 | tf_op jit(solution)/shard_map/psum | solution.py:60
  82.0 0.0 copy-done.1
  82.0 3.1 %fusion.7 = bf16[2,24,8,32]{3,2,1,0:T(8,128)(2,1)S(1)} fusion(f32[2,24,3,8,32]{4,3,1,0,2:T(8,128)} %all-reduce.3.cloned.1.call-done, f32[24,32]{1,0:T(8,128)S(1)} %copy-done.1, f32[]{:T(128)} %bitcast.6, f32[]{:T(128)} %bitcast.5, f32[]{:T(128)} %bitcast.4), kind=kLoop, calls=%fused_computation.13 | loop fusion | flops 86016 | bytes 175116 | tf_op jit(solution)/shard_map/convert_element_type | solution.py:32
  85.1 0.4 fusion
  85.5 0.4 fusion.2
  85.9 0.4 fusion.1
  86.3 0.7 multiply_reduce_fusion
  87.0 0.1 reshape.98
  87.1 0.1 reduce_sum.35
  87.2 8.9 %all-reduce = f32[24,8]{0,1:T(8,128)S(1)} all-reduce(f32[24,8]{0,1:T(8,128)S(1)} %multiply_bitcast_fusion), channel_id=2, replica_groups=mesh['re'=4,'ka'=8] {'re'}, use_global_device_ids=true, to_apply=%region_4.5.clone | all-reduce | flops 192 | bytes 1536
  96.1 0.6 constant_dynamic-slice_fusion
  (6 shorter events, 0.1 us)
Async XLA Ops:
  6.5 75.5 %all-reduce.3.cloned.1.call-start = ((), (), s32[]{:S(2)}) async-start(), calls=%async_computation | async-start | bytes 1179648 | tf_op jit(solution)/shard_map/psum | solution.py:60
  36.2 1.4 %copy-start = (bf16[1,24,2,32,8]{3,4,2,1,0:T(8,128)(2,1)S(1)}, bf16[1,24,2,32,8]{3,4,2,1,0:T(8,128)(2,1)}, u32[]{:S(2)}) copy-start(bf16[1,24,2,32,8]{3,4,2,1,0:T(8,128)(2,1)} %param.12) | copy-start | bytes 73732
  36.7 17.2 %copy-start.3 = (bf16[1,24]{1,0:T(2,128)(2,1)S(1)}, bf16[1,24]{1,0:T(2,128)(2,1)}, u32[]{:S(2)}) copy-start(bf16[1,24]{1,0:T(2,128)(2,1)} %param.13) | copy-start | bytes 148
  36.7 25.9 %copy-start.4 = (u32[32]{0:T(128)S(1)}, u32[32]{0:T(128)}, u32[]{:S(2)}) copy-start(u32[32]{0:T(128)} %constant.28) | copy-start | bytes 388
  36.7 27.2 %copy-start.2 = (f32[3]{0:T(128)S(1)}, f32[3]{0:T(128)}, u32[]{:S(2)}) copy-start(f32[3]{0:T(128)} %param.10) | copy-start | bytes 40
  36.8 45.3 %copy-start.1 = (f32[24,32]{1,0:T(8,128)S(1)}, f32[24,32]{1,0:T(8,128)}, u32[]{:S(2)}) copy-start(f32[24,32]{1,0:T(8,128)} %param.11) | copy-start | bytes 9220
Sparse Core Ops, SparseCore 0:
  37.8 44.1 all-reduce.2
where the time goes:
time: 104 us
  blocking collectives  61.6 us (59%)
  waiting for transfers between devices  17.5 us (17%)
  between operations  14.2 us (14%)
  other arithmetic  4.75 us (5%)
  local copies, waits for them, and re-layouts  3.38 us (3%)
  matrix products  2.13 us (2%)
    psum x1, waiting for transfers between devices, body(): momenta = lax.psum(partial_value, 're').reshape(2, own_count, cols)  17.4 us
    all_gather x1, blocking collectives, body(): lax.all_gather(coupling, 'ka', axis=0, tiled=True)  16.3 us
    all_gather x1, blocking collectives, body(): blocks = lax.all_gather(lattice_blocks, 'ka', axis=0, tiled=True)  14.2 us
    all_gather x1, blocking collectives, body(): lax.all_gather(lattice_coords.astype(jnp.bfloat16), 'ka', axis=0, tiled=T...  13.5 us
    unnamed x1, blocking collectives  8.93 us
    all_gather x1, blocking collectives, body(): lax.all_gather(phonon_weight, 'ka', axis=0, tiled=True)  8.72 us
    convert_element_type x1, other arithmetic, left_factor(): (along / energy_gap[None, :, None, :]).astype(jnp.bfloat16)  3.05 us
  transfers between devices with their start and end apart: 1, of which 1 were waited for; matrix products, arithmetic and copies ran while one was open for 1% of the time, Pallas kernels for 0%

commit v1 on v0

--- a/solution.py
+++ b/solution.py
@@ -53,7 +53,12 @@
 ):
     own_count = kpoint_index.shape[0]
     cols = lattice_blocks.shape[2] * lattice_blocks.shape[3]
-    blocks = lax.all_gather(lattice_blocks, "ka", axis=0, tiled=True)
+    ring = [lattice_blocks]
+    for hop in range(7):
+        ring.append(lax.ppermute(ring[-1], "ka", [(dev, (dev + 1) % 8) for dev in range(8)]))
+    blocks = jnp.roll(
+        jnp.concatenate(ring[::-1], axis=0), (lax.axis_index("ka") + 1) * ring[0].shape[0], axis=0
+    )
     coords = lax.all_gather(lattice_coords.astype(jnp.bfloat16), "ka", axis=0, tiled=True)
     left = phase_rows(kpoint_index, coords.astype(jnp.int32))
     partial_value = jnp.dot(left, blocks.reshape(-1, cols), preferred_element_type=jnp.float32)

time: 104 us -> 119 us (1.14)
  waiting for transfers between devices: 17.5 us -> 45.8 us
  blocking collectives: 61.6 us -> 44.4 us
  local copies, waits for them, and re-layouts: 3.38 us -> 6.11 us
    ppermute x0 -> x7, waiting for transfers between devices: none -> 28.1 us  [body(): lax.ppermute(ring[-1], 'ka', [(dev, (dev + 1) % 8) for dev in range(8)])]
    all_gather x1 -> x0, blocking collectives: 14.2 us -> none  [body(): blocks = lax.all_gather(lattice_blocks, 'ka', axis=0, tiled=True)]
    all_gather x1, blocking collectives: 13.5 us -> 10.7 us  [body(): lax.all_gather(lattice_coords.astype(jnp.bfloat16), 'ka', axis=0, tiled=T...]
    unnamed x14 -> x27, local copies, waits for them, and re-layouts: 1.23 us -> 3.16 us
  transfers between devices with their start and end apart: 1 -> 8, of which waited for: 1 -> 7; matrix products, arithmetic and copies ran while one was open for 1% -> 3% of each run, Pallas kernels for 0% -> 0%
where the time goes in v1:
time: 119 us; the launch traced here: 118 us
  waiting for transfers between devices  45.8 us (38%)
  blocking collectives  44.4 us (37%)
  between operations  14.3 us (12%)
  local copies, waits for them, and re-layouts  6.11 us (5%)
  other arithmetic  4.71 us (4%)
  matrix products  2.13 us (2%)
    ppermute x7, waiting for transfers between devices, body(): lax.ppermute(ring[-1], 'ka', [(dev, (dev + 1) % 8) for dev in range(8)])  28.1 us
    psum x1, waiting for transfers between devices, body(): momenta = lax.psum(partial_value, 're').reshape(2, own_count, cols)  17.7 us
    all_gather x1, blocking collectives, body(): lax.all_gather(coupling, 'ka', axis=0, tiled=True)  15.7 us
    all_gather x1, blocking collectives, body(): lax.all_gather(lattice_coords.astype(jnp.bfloat16), 'ka', axis=0, tiled=T...  10.7 us
    all_gather x1, blocking collectives, body(): lax.all_gather(phonon_weight, 'ka', axis=0, tiled=True)  9.09 us
    unnamed x1, blocking collectives  8.94 us
    unnamed x27, local copies, waits for them, and re-layouts  3.16 us
    convert_element_type x1, other arithmetic, left_factor(): (along / energy_gap[None, :, None, :]).astype(jnp.bfloat16)  3.02 us
  transfers between devices with their start and end apart: 8, of which 7 were waited for; matrix products, arithmetic and copies ran while one was open for 3% of the time, Pallas kernels for 0%

profile of v1, /device:TPU:0, one launch (start us, length us, event | category | flops | bytes accessed | tf_op | source)
XLA Modules:
  0.0 118.3 jit_solution(17723839264477893963)
XLA Ops:
  6.5 0.0 all-reduce.3.cloned.1.call-start
  6.5 0.5 collective-permute-start
  7.0 5.7 %collective-permute-done = bf16[6,2,3,256]{3,1,2,0:T(2,128)(2,1)S(1)} collective-permute-done((bf16[6,2,3,256]{3,1,2,0:T(2,128)(2,1)}, bf16[6,2,3,256]{3,1,2,0:T(2,128)(2,1)S(1)}, u32[]{:S(2)}, u32[]{:S(2)}) %collective-permute-start) | collective-permute-done | bytes 18464 | tf_op jit(solution)/shard_map/ppermute | solution.py:58
  12.7 0.0 collective-permute-start.1
  12.7 0.7 convert_bitcast_fusion
  13.4 10.7 %all-gather = bf16[8,6,3]{1,2,0:T(4,128)(2,1)S(1)} all-gather(bf16[1,6,3]{1,2,0:T(4,128)(2,1)S(1)} %convert_bitcast_fusion), channel_id=1, replica_groups=mesh['re'=4,'ka'=8] {'ka'}, dimensions={0}, use_global_device_ids=true | all-gather | bytes 324 | tf_op jit(solution)/shard_map/all_gather | solution.py:62
  24.1 0.0 collective-permute-done.1
  24.1 0.3 collective-permute-start.2
  24.4 0.1 reshape.103
  24.5 4.6 %collective-permute-done.2 = bf16[6,2,3,256]{3,1,2,0:T(2,128)(2,1)S(1)} collective-permute-done((bf16[6,2,3,256]{3,1,2,0:T(2,128)(2,1)S(1)}, bf16[6,2,3,256]{3,1,2,0:T(2,128)(2,1)S(1)}, u32[]{:S(2)}, u32[]{:S(2)}) %collective-permute-start.2) | collective-permute-done | bytes 18464 | tf_op jit(solution)/shard_map/ppermute | solution.py:58
  29.1 0.0 collective-permute-start.3
  29.1 0.8 multiply_reduce_fusion.1
  29.8 4.2 %collective-permute-done.3 = bf16[6,2,3,256]{3,1,2,0:T(2,128)(2,1)S(1)} collective-permute-done((bf16[6,2,3,256]{3,1,2,0:T(2,128)(2,1)S(1)}, bf16[6,2,3,256]{3,1,2,0:T(2,128)(2,1)S(1)}, u32[]{:S(2)}, u32[]{:S(2)}) %collective-permute-start.3) | collective-permute-done | bytes 18464 | tf_op jit(solution)/shard_map/ppermute | solution.py:58
  34.1 0.0 collective-permute-start.4
  34.1 0.1 fusion.16
  34.1 4.9 %collective-permute-done.4 = bf16[6,2,3,256]{3,1,2,0:T(2,128)(2,1)S(1)} collective-permute-done((bf16[6,2,3,256]{3,1,2,0:T(2,128)(2,1)S(1)}, bf16[6,2,3,256]{3,1,2,0:T(2,128)(2,1)S(1)}, u32[]{:S(2)}, u32[]{:S(2)}) %collective-permute-start.4) | collective-permute-done | bytes 18464 | tf_op jit(solution)/shard_map/ppermute | solution.py:58
  39.0 0.0 collective-permute-start.5
  39.0 0.1 cosine_convert_fusion
  39.1 4.9 %collective-permute-done.5 = bf16[6,2,3,256]{3,1,2,0:T(2,128)(2,1)S(1)} collective-permute-done((bf16[6,2,3,256]{3,1,2,0:T(2,128)(2,1)S(1)}, bf16[6,2,3,256]{3,1,2,0:T(2,128)(2,1)S(1)}, u32[]{:S(2)}, u32[]{:S(2)}) %collective-permute-start.5) | collective-permute-done | bytes 18464 | tf_op jit(solution)/shard_map/ppermute | solution.py:58
  44.0 0.0 collective-permute-start.6
  44.1 0.1 copy.53
  44.2 0.1 copy.54
  44.3 0.9 copy.57
  45.2 3.8 %collective-permute-done.6 = bf16[6,2,3,256]{3,1,2,0:T(2,128)(2,1)S(1)} collective-permute-done((bf16[6,2,3,256]{3,1,2,0:T(2,128)(2,1)S(1)}, bf16[6,2,3,256]{3,1,2,0:T(2,128)(2,1)S(1)}, u32[]{:S(2)}, u32[]{:S(2)}) %collective-permute-start.6) | collective-permute-done | bytes 18464 | tf_op jit(solution)/shard_map/ppermute | solution.py:58
  49.2 0.7 constant_dynamic-update-slice_fusion.8
  50.1 0.7 constant_dynamic-update-slice_fusion
  50.9 0.1 constant_dynamic-slice_fusion.1
  51.0 0.1 copy.55
  51.1 0.3 fusion.8
  51.4 0.0 copy-start.2
  51.4 0.0 copy-start.3
  51.4 0.0 copy-start.1
  51.4 0.0 copy-start
  51.4 0.2 reshape_reshape.3
  51.6 0.8 copy.56
  52.5 0.0 all-reduce.3.cloned.1.call-update
  52.5 15.7 %all_gather.10 = bf16[8,24,2,32,8]{3,1,4,0,2:T(8,128)(2,1)S(1)} all-gather(bf16[1,24,2,32,8]{3,1,4,0,2:T(8,128)(2,1)S(1)} %copy.57), channel_id=1, replica_groups=mesh['re'=4,'ka'=8] {'ka'}, dimensions={0}, use_global_device_ids=true | all-gather | bytes 221184 | tf_op jit(solution)/shard_map/all_gather | solution.py:69
  68.2 0.0 copy-done.2
  68.2 9.1 %all-gather.1 = bf16[8,1,24]{2,1,0:T(2,128)(2,1)S(1)} all-gather(bf16[1,1,24]{2,1,0:T(2,128)(2,1)S(1)} %bitcast.62), channel_id=1, replica_groups=mesh['re'=4,'ka'=8] {'ka'}, dimensions={0}, use_global_device_ids=true | all-gather | bytes 432 | tf_op jit(solution)/shard_map/all_gather | solution.py:70
  77.3 0.0 copy-done.3
  77.3 0.6 dynamic-slice
  78.5 0.0 copy-done.1
  78.6 0.6 fusion.17
  79.2 17.7 %all-reduce.3.cloned.1.call-done = f32[2,24,3,8,32]{4,3,1,0,2:T(8,128)} async-done(((f32[2,24,3,8,32]{4,3,1,0,2:T(8,128)}), f32[2,24,3,8,32]{4,3,1,0,2:T(8,128)}) %all-reduce.3.cloned.1.call-update) | async-done | bytes 147472 | tf_op jit(solution)/shard_map/psum | solution.py:65
  96.8 0.0 copy-done
  96.8 3.0 %fusion.7 = bf16[2,24,8,32]{3,2,1,0:T(8,128)(2,1)S(1)} fusion(f32[2,24,3,8,32]{4,3,1,0,2:T(8,128)} %all-reduce.3.cloned.1.call-done, f32[24,32]{1,0:T(8,128)S(1)} %copy-done, f32[]{:T(128)} %bitcast.6, f32[]{:T(128)} %bitcast.5, f32[]{:T(128)} %bitcast.4), kind=kLoop, calls=%fused_computation.13 | loop fusion | flops 86016 | bytes 175116 | tf_op jit(solution)/shard_map/convert_element_type | solution.py:32
  99.9 0.4 fusion
  100.3 0.4 fusion.2
  100.7 0.4 fusion.1
  101.1 0.7 multiply_reduce_fusion
  101.8 0.1 reshape.98
  101.9 0.1 reduce_sum.35
  102.0 8.9 %all-reduce = f32[24,8]{0,1:T(8,128)S(1)} all-reduce(f32[24,8]{0,1:T(8,128)S(1)} %multiply_bitcast_fusion), channel_id=2, replica_groups=mesh['re'=4,'ka'=8] {'re'}, use_global_device_ids=true, to_apply=%region_4.5.clone | all-reduce | flops 192 | bytes 1536
  110.9 0.6 constant_dynamic-slice_fusion
  (19 shorter events, 0.3 us)
Async XLA Ops:
  6.5 90.3 %all-reduce.3.cloned.1.call-start = ((), (), s32[]{:S(2)}) async-start(), calls=%async_computation | async-start | bytes 1179648 | tf_op jit(solution)/shard_map/psum | solution.py:65
  6.5 6.2 %collective-permute-start = (bf16[6,2,3,256]{3,1,2,0:T(2,128)(2,1)}, bf16[6,2,3,256]{3,1,2,0:T(2,128)(2,1)S(1)}, u32[]{:S(2)}, u32[]{:S(2)}) collective-permute-start(bf16[6,2,3,256]{3,1,2,0:T(2,128)(2,1)} %param.7), channel_id=1, source_target_pairs={{0,1},{1,2},{2,3},{3,4},{4,5},{5,6},{6,7},{7,0},{8,9},{9,10},{10,1... | collective-permute-start | bytes 55304 | tf_op jit(solution)/shard_map/ppermute | solution.py:58
  12.7 11.4 %collective-permute-start.1 = (bf16[6,2,3,256]{3,1,2,0:T(2,128)(2,1)S(1)}, bf16[6,2,3,256]{3,1,2,0:T(2,128)(2,1)S(1)}, u32[]{:S(2)}, u32[]{:S(2)}) collective-permute-start(bf16[6,2,3,256]{3,1,2,0:T(2,128)(2,1)S(1)} %collective-permute-done), channel_id=1, source_target_pairs={{0,1},{1,2},{2,3},{3,4},{4,5},{5,6},{6,7},{7,0},{8,9},{9,10},{10,1... | collective-permute-start | bytes 55304 | tf_op jit(solution)/shard_map/ppermute | solution.py:58
  24.1 5.0 %collective-permute-start.2 = (bf16[6,2,3,256]{3,1,2,0:T(2,128)(2,1)S(1)}, bf16[6,2,3,256]{3,1,2,0:T(2,128)(2,1)S(1)}, u32[]{:S(2)}, u32[]{:S(2)}) collective-permute-start(bf16[6,2,3,256]{3,1,2,0:T(2,128)(2,1)S(1)} %collective-permute-done.1), channel_id=1, source_target_pairs={{0,1},{1,2},{2,3},{3,4},{4,5},{5,6},{6,7},{7,0},{8,9},{9,10},{10,1... | collective-permute-start | bytes 55304 | tf_op jit(solution)/shard_map/ppermute | solution.py:58
  29.1 5.0 %collective-permute-start.3 = (bf16[6,2,3,256]{3,1,2,0:T(2,128)(2,1)S(1)}, bf16[6,2,3,256]{3,1,2,0:T(2,128)(2,1)S(1)}, u32[]{:S(2)}, u32[]{:S(2)}) collective-permute-start(bf16[6,2,3,256]{3,1,2,0:T(2,128)(2,1)S(1)} %collective-permute-done.2), channel_id=1, source_target_pairs={{0,1},{1,2},{2,3},{3,4},{4,5},{5,6},{6,7},{7,0},{8,9},{9,10},{10,1... | collective-permute-start | bytes 55304 | tf_op jit(solution)/shard_map/ppermute | solution.py:58
  34.1 5.0 %collective-permute-start.4 = (bf16[6,2,3,256]{3,1,2,0:T(2,128)(2,1)S(1)}, bf16[6,2,3,256]{3,1,2,0:T(2,128)(2,1)S(1)}, u32[]{:S(2)}, u32[]{:S(2)}) collective-permute-start(bf16[6,2,3,256]{3,1,2,0:T(2,128)(2,1)S(1)} %collective-permute-done.3), channel_id=1, source_target_pairs={{0,1},{1,2},{2,3},{3,4},{4,5},{5,6},{6,7},{7,0},{8,9},{9,10},{10,1... | collective-permute-start | bytes 55304 | tf_op jit(solution)/shard_map/ppermute | solution.py:58
  39.0 5.0 %collective-permute-start.5 = (bf16[6,2,3,256]{3,1,2,0:T(2,128)(2,1)S(1)}, bf16[6,2,3,256]{3,1,2,0:T(2,128)(2,1)S(1)}, u32[]{:S(2)}, u32[]{:S(2)}) collective-permute-start(bf16[6,2,3,256]{3,1,2,0:T(2,128)(2,1)S(1)} %collective-permute-done.4), channel_id=1, source_target_pairs={{0,1},{1,2},{2,3},{3,4},{4,5},{5,6},{6,7},{7,0},{8,9},{9,10},{10,1... | collective-permute-start | bytes 55304 | tf_op jit(solution)/shard_map/ppermute | solution.py:58
  44.0 5.0 %collective-permute-start.6 = (bf16[6,2,3,256]{3,1,2,0:T(2,128)(2,1)S(1)}, bf16[6,2,3,256]{3,1,2,0:T(2,128)(2,1)S(1)}, u32[]{:S(2)}, u32[]{:S(2)}) collective-permute-start(bf16[6,2,3,256]{3,1,2,0:T(2,128)(2,1)S(1)} %collective-permute-done.5), channel_id=1, source_target_pairs={{0,1},{1,2},{2,3},{3,4},{4,5},{5,6},{6,7},{7,0},{8,9},{9,10},{10,1... | collective-permute-start | bytes 55304 | tf_op jit(solution)/shard_map/ppermute | solution.py:58
  51.4 16.9 %copy-start.2 = (bf16[1,24]{1,0:T(2,128)(2,1)S(1)}, bf16[1,24]{1,0:T(2,128)(2,1)}, u32[]{:S(2)}) copy-start(bf16[1,24]{1,0:T(2,128)(2,1)} %param.13) | copy-start | bytes 148
  51.4 25.9 %copy-start.3 = (u32[32]{0:T(128)S(1)}, u32[32]{0:T(128)}, u32[]{:S(2)}) copy-start(u32[32]{0:T(128)} %constant.54) | copy-start | bytes 388
  51.4 27.2 %copy-start.1 = (f32[3]{0:T(128)S(1)}, f32[3]{0:T(128)}, u32[]{:S(2)}) copy-start(f32[3]{0:T(128)} %param.10) | copy-start | bytes 40
  51.4 45.5 %copy-start = (f32[24,32]{1,0:T(8,128)S(1)}, f32[24,32]{1,0:T(8,128)}, u32[]{:S(2)}) copy-start(f32[24,32]{1,0:T(8,128)} %param.11) | copy-start | bytes 9220
Sparse Core Ops, SparseCore 0:
  52.6 44.1 all-reduce.2
